TPU v7x, 32 devices: a whole 2x2x4 slice. The times are simulated.
32 devices in a mesh: prow: 4 (over y, x), pcol: 8 (over z, core).
Axes of the slice: x: 2, y: 2, z: 4, core: 2. Of those that a mesh axis runs over, the one named last changes fastest.
Arguments:
- panel_t: float32 [8, 256, 4096], P('pcol', None, 'prow'), may hold values from -0.09375 to 0.09375
- ancestor: float32 [4096, 4096], P('prow', 'pcol'), as said below
- structure: int32 [8, 16], replicated, may hold values 0 or 1
- diag_inv: float32 [8, 256, 256], P('pcol'), may hold values from -6 to 6
Outputs:
- inverse_panel: float32 [2048, 4096], P('pcol', 'prow')
- inverse_diag: float32 [8, 256, 256], P('pcol')
Inputs may be any that keep to these rules, and one draw needn't show every extreme that they name: ancestor is symmetric up to rounding.
All inputs are finite; a program needn't handle non-finite values.
Results may differ from a plain program's by a relative error of at most 0.00007.
Values sent between devices are 32-bit elements; how exact they have to be, the bound alone decides.
A program may use at most 128 MiB of HBM per device.

v0:
```python
import jax
import jax.numpy as jnp
from jax import lax
from jax.sharding import PartitionSpec as P


def local(panel_t, ancestor, structure, diag_inv):
    local_sn = panel_t.shape[0]
    width = panel_t.shape[1]
    row_span = panel_t.shape[2]
    row_blocks = row_span // width
    col_index = lax.axis_index("pcol")
    row_index = lax.axis_index("prow")
    mine = lax.dynamic_slice(
        structure, (col_index * local_sn, row_index * row_blocks), (local_sn, row_blocks)
    )
    masked = (
        panel_t.reshape(local_sn, width, row_blocks, width)
        * mine.astype(jnp.float32)[:, None, :, None]
    )
    masked = masked.reshape(local_sn, width, row_span)
    prow_size = lax.axis_size("prow")
    rows_here = width // prow_size
    arranged = masked.reshape(local_sn, prow_size, rows_here, row_span).transpose(1, 0, 2, 3)
    gathered = lax.all_gather(arranged, "pcol", axis=1, tiled=True)
    total_nodes = gathered.shape[1]
    flat_rows = gathered.reshape(prow_size * total_nodes * rows_here, row_span)
    reduced = lax.psum_scatter(
        jnp.dot(
            flat_rows, ancestor, precision=lax.Precision.HIGHEST, preferred_element_type=jnp.float32
        ),
        "prow",
        scatter_dimension=0,
        tiled=True,
    )
    moved = lax.all_to_all(
        lax.all_to_all(reduced, "pcol", split_axis=0, concat_axis=1, tiled=True),
        "prow",
        split_axis=1,
        concat_axis=0,
        tiled=True,
    )
    summed = moved.reshape(prow_size, local_sn, rows_here, row_span).transpose(1, 0, 2, 3)
    summed = summed.reshape(local_sn * width, row_span)
    inverse_panel = -summed
    blocks = inverse_panel.reshape(local_sn, width, row_span)
    partial_diag = jnp.einsum("kbj,kcj->kbc", blocks, masked, precision=lax.Precision.HIGHEST)
    inverse_diag = diag_inv - lax.psum(partial_diag, "prow")
    return (inverse_panel, inverse_diag)


def solution(mesh):
    return jax.shard_map(
        local,
        mesh=mesh,
        in_specs=(P("pcol", None, "prow"), P("prow", "pcol"), P(), P("pcol", None, None)),
        out_specs=(P("pcol", "prow"), P("pcol", None, None)),
        check_vma=False,
    )
```

profile of v0, /device:TPU:0, one launch (start us, length us, event | category | flops | bytes accessed | tf_op | source)
XLA Modules:
  0.0 269.8 jit_solution(682398275534982507)
XLA Ops:
  7.2 0.0 copy-start
  7.2 0.0 all-gather.2.cloned.1.call-start
  7.2 0.9 convert_bitcast_fusion
  8.1 0.1 broadcast_bitcast_fusion
  8.2 2.3 broadcast_multiply_fusion
  10.5 0.0 all-gather.2.cloned.1.call-update
  10.5 0.0 reduce-scatter.2.cloned.1.call-start
  10.6 84.9 %all-gather.2.cloned.1.call-done = f32[4,8,64,1024]{3,2,1,0:T(8,128)} async-done(((f32[4,1,64,1024]{3,2,1,0:T(8,128)}), f32[4,8,64,1024]{3,2,1,0:T(8,128)}) %all-gather.2.cloned.1.call-update) | async-done | bytes 8388624 | tf_op jit(solution)/shard_map/all_gather | solution.py:25
  95.5 0.0 copy-done
  95.5 16.9 %fusion.3 = f32[2048,512]{1,0:T(8,128)} fusion(f32[2048,1024]{1,0:T(8,128)} %bitcast.27, f32[1024,512]{1,0:T(8,128)S(1)} %copy-done), kind=kOutput, calls=%fused_computation.7 | convolution fusion | flops 12884901888 | bytes 14680064 | tf_op jit(solution)/shard_map/dot_general | solution.py:29
  112.3 0.0 reduce-scatter.2.cloned.1.call-update
  112.4 0.0 all-reduce.2.cloned.1.call-start
  112.4 51.2 %reduce-scatter.2.cloned.1.call-done = f32[512,512]{1,0:T(8,128)} async-done(((f32[2048,512]{1,0:T(8,128)}), f32[512,512]{1,0:T(8,128)}) %reduce-scatter.2.cloned.1.call-update) | async-done | bytes 1048592 | tf_op jit(solution)/shard_map/reduce_scatter | solution.py:28
  163.6 31.2 %all_to_all.29 = f32[8,64,512]{2,1,0:T(8,128)S(1)} all-to-all(f32[8,64,512]{2,1,0:T(8,128)} %bitcast.24), channel_id=1, replica_groups=mesh['prow'=4,'pcol'=8] {'pcol'}, dimensions={0} | all-to-all | bytes 2097152 | tf_op jit(solution)/shard_map/all_to_all | solution.py:37
  194.8 1.6 copy.9
  196.4 0.0 copy-start.1
  196.4 2.8 %all_to_all.25 = f32[64,4,1024]{2,1,0:T(4,128)} reshape(f32[64,8,512]{2,1,0:T(8,128)} %copy.9) | data formatting | bytes 2097152 | tf_op jit(solution)/shard_map/all_to_all | solution.py:36
  199.2 0.0 copy-start.3
  199.2 1.9 copy.10
  201.0 16.5 %all_to_all.30 = f32[64,4,1024]{2,0,1:T(8,128)S(1)} all-to-all(f32[64,4,1024]{2,0,1:T(8,128)S(1)} %copy.10), channel_id=1, replica_groups=mesh['prow'=4,'pcol'=8] {'prow'}, dimensions={1} | all-to-all | bytes 2097152 | tf_op jit(solution)/shard_map/all_to_all | solution.py:36
  217.5 0.1 neg.13
  217.6 0.0 copy-start.2
  217.6 1.0 copy-done.2
  218.6 0.0 copy-done.1
  218.6 1.8 convolution_bitcast_fusion
  220.4 0.0 all-reduce.2.cloned.1.call-update
  220.4 41.2 %all-reduce.2.cloned.1.call-done = f32[1,256,256]{2,1,0:T(8,128)} async-done(((f32[1,256,256]{2,1,0:T(8,128)}), f32[1,256,256]{2,1,0:T(8,128)}) %all-reduce.2.cloned.1.call-update) | async-done | bytes 262160 | tf_op jit(solution)/shard_map/psum | solution.py:48
  261.6 0.0 copy-done.3
  261.6 1.7 sub.3
  (1 shorter events, 0.0 us)
Async XLA Ops:
  7.2 88.3 %copy-start = (f32[1024,512]{1,0:T(8,128)S(1)}, f32[1024,512]{1,0:T(8,128)}, u32[]{:S(2)}) copy-start(f32[1024,512]{1,0:T(8,128)} %param.5) | copy-start | bytes 6291460
  7.2 88.3 %all-gather.2.cloned.1.call-start = ((), (), s32[]{:S(2)}) async-start(), calls=%async_computation.3 | async-start | bytes 9437184 | tf_op jit(solution)/shard_map/all_gather | solution.py:25
  10.5 153.1 %reduce-scatter.2.cloned.1.call-start = ((), (), s32[]{:S(2)}) async-start(), calls=%async_computation.4 | async-start | bytes 5242880 | tf_op jit(solution)/shard_map/reduce_scatter | solution.py:28
  112.4 149.2 %all-reduce.2.cloned.1.call-start = ((), (), s32[]{:S(2)}) async-start(), calls=%async_computation.5 | async-start | bytes 524288 | tf_op jit(solution)/shard_map/psum | solution.py:48
  196.4 22.2 %copy-start.1 = (f32[1,256,1024]{2,1,0:T(8,128)S(1)}, f32[1,256,1024]{2,1,0:T(8,128)}, u32[]{:S(2)}) copy-start(f32[1,256,1024]{2,1,0:T(8,128)} %param.4) | copy-start | bytes 3145732
  199.2 62.4 %copy-start.3 = (f32[1,256,256]{2,1,0:T(8,128)S(1)}, f32[1,256,256]{2,1,0:T(8,128)}, u32[]{:S(2)}) copy-start(f32[1,256,256]{2,1,0:T(8,128)} %param.7) | copy-start | bytes 786436
  217.6 1.0 copy-start.2
Sparse Core Ops, SparseCore 0:
  10.7 84.7 all-gather.1
  112.5 51.0 reduce-scatter.1
  220.5 41.0 all-reduce.1
where the time goes:
time: 270 us
  waiting for transfers between devices  177 us (66%)
  blocking collectives  47.6 us (18%)
  matrix products  18.6 us (7%)
  between operations  13.8 us (5%)
  local copies, waits for them, and re-layouts  7.31 us (3%)
  other arithmetic  5.02 us (2%)
    all_gather x1, waiting for transfers between devices, local(): gathered = lax.all_gather(arranged, 'pcol', axis=1, tiled=True)  84.9 us
    reduce_scatter x1, waiting for transfers between devices, local(): lax.psum_scatter(jnp.dot(flat_rows, ancestor, precision=lax.Precision.HIG...  51.2 us
    psum x1, waiting for transfers between devices, local(): inverse_diag = diag_inv - lax.psum(partial_diag, 'prow')  41.2 us
    all_to_all x1, blocking collectives, local(): lax.all_to_all(reduced, 'pcol', split_axis=0, concat_axis=1, tiled=True)  31.2 us
    dot_general x1, matrix products, local(): jnp.dot(flat_rows, ancestor, precision=lax.Precision.HIGHEST, preferred_e...  16.9 us
    all_to_all x1, blocking collectives, local(): lax.all_to_all(lax.all_to_all(reduced, 'pcol', split_axis=0, concat_axis=...  16.5 us
  transfers between devices with their start and end apart: 3, of which 3 were waited for; matrix products, arithmetic and copies ran while one was open for 0% of the time, Pallas kernels for 0%

commit v1 on v0

--- a/solution.py
+++ b/solution.py
@@ -45,7 +45,7 @@
     inverse_panel = -summed
     blocks = inverse_panel.reshape(local_sn, width, row_span)
     partial_diag = jnp.einsum("kbj,kcj->kbc", blocks, masked, precision=lax.Precision.HIGHEST)
-    inverse_diag = diag_inv - lax.psum(partial_diag, "prow")
+    inverse_diag = diag_inv - jnp.sum(lax.all_gather(partial_diag, "prow"), axis=0)
     return (inverse_panel, inverse_diag)
 
 

time: 270 us -> 254 us (0.941)
  waiting for transfers between devices: 177 us -> 161 us
    psum x1 -> x0, waiting for transfers between devices: 41.2 us -> none  [local(): inverse_diag = diag_inv - lax.psum(partial_diag, 'prow')]
    all_gather x0 -> x1, waiting for transfers between devices: none -> 24.6 us  [local(): lax.all_gather(partial_diag, 'prow')]
where the time goes in v1:
time: 254 us
  waiting for transfers between devices  161 us (63%)
  blocking collectives  47.8 us (19%)
  matrix products  18.6 us (7%)
  between operations  13.8 us (5%)
  local copies, waits for them, and re-layouts  7.27 us (3%)
  other arithmetic  5.42 us (2%)
    all_gather x1, waiting for transfers between devices, local(): gathered = lax.all_gather(arranged, 'pcol', axis=1, tiled=True)  84.9 us
    reduce_scatter x1, waiting for transfers between devices, local(): lax.psum_scatter(jnp.dot(flat_rows, ancestor, precision=lax.Precision.HIG...  51.2 us
    all_to_all x1, blocking collectives, local(): lax.all_to_all(reduced, 'pcol', split_axis=0, concat_axis=1, tiled=True)  31.2 us
    all_gather x1, waiting for transfers between devices, local(): lax.all_gather(partial_diag, 'prow')  24.6 us
    dot_general x1, matrix products, local(): jnp.dot(flat_rows, ancestor, precision=lax.Precision.HIGHEST, preferred_e...  16.9 us
    all_to_all x1, blocking collectives, local(): lax.all_to_all(lax.all_to_all(reduced, 'pcol', split_axis=0, concat_axis=...  16.6 us
  transfers between devices with their start and end apart: 3, of which 3 were waited for; matrix products, arithmetic and copies ran while one was open for 0% of the time, Pallas kernels for 0%

profile of v1, /device:TPU:0, one launch (start us, length us, event | category | flops | bytes accessed | tf_op | source)
XLA Modules:
  0.0 253.8 jit_solution(203688385634127160)
XLA Ops:
  7.2 0.0 copy-start
  7.2 0.0 all-gather.4.cloned.1.call-start
  7.2 0.9 convert_bitcast_fusion
  8.1 0.1 broadcast_bitcast_fusion
  8.2 2.3 broadcast_multiply_fusion
  10.6 0.0 all-gather.4.cloned.1.call-update
  10.6 0.0 reduce-scatter.2.cloned.1.call-start
  10.6 84.9 %all-gather.4.cloned.1.call-done = f32[4,8,64,1024]{3,2,1,0:T(8,128)} async-done(((f32[4,1,64,1024]{3,2,1,0:T(8,128)}), f32[4,8,64,1024]{3,2,1,0:T(8,128)}) %all-gather.4.cloned.1.call-update) | async-done | bytes 8388624 | tf_op jit(solution)/shard_map/all_gather | solution.py:25
  95.5 0.0 copy-done
  95.5 16.9 %fusion.4 = f32[2048,512]{1,0:T(8,128)} fusion(f32[2048,1024]{1,0:T(8,128)} %bitcast.29, f32[1024,512]{1,0:T(8,128)S(1)} %copy-done), kind=kOutput, calls=%fused_computation.8 | convolution fusion | flops 12884901888 | bytes 14680064 | tf_op jit(solution)/shard_map/dot_general | solution.py:29
  112.4 0.0 reduce-scatter.2.cloned.1.call-update
  112.4 0.0 all-gather.6.cloned.1.call-start
  112.5 51.2 %reduce-scatter.2.cloned.1.call-done = f32[512,512]{1,0:T(8,128)} async-done(((f32[2048,512]{1,0:T(8,128)}), f32[512,512]{1,0:T(8,128)}) %reduce-scatter.2.cloned.1.call-update) | async-done | bytes 1048592 | tf_op jit(solution)/shard_map/reduce_scatter | solution.py:28
  163.7 31.2 %all_to_all.29 = f32[8,64,512]{2,1,0:T(8,128)S(1)} all-to-all(f32[8,64,512]{2,1,0:T(8,128)} %bitcast.26), channel_id=1, replica_groups=mesh['prow'=4,'pcol'=8] {'pcol'}, dimensions={0} | all-to-all | bytes 2097152 | tf_op jit(solution)/shard_map/all_to_all | solution.py:37
  194.8 1.6 copy.9
  196.4 0.0 copy-start.1
  196.4 2.8 %all_to_all.25 = f32[64,4,1024]{2,1,0:T(4,128)} reshape(f32[64,8,512]{2,1,0:T(8,128)} %copy.9) | data formatting | bytes 2097152 | tf_op jit(solution)/shard_map/all_to_all | solution.py:36
  199.2 1.8 copy.10
  201.0 0.0 copy-start.3
  201.0 16.6 %all_to_all.30 = f32[64,4,1024]{2,0,1:T(8,128)S(1)} all-to-all(f32[64,4,1024]{2,0,1:T(8,128)S(1)} %copy.10), channel_id=1, replica_groups=mesh['prow'=4,'pcol'=8] {'prow'}, dimensions={1} | all-to-all | bytes 2097152 | tf_op jit(solution)/shard_map/all_to_all | solution.py:36
  217.6 0.1 neg.13
  217.8 0.0 copy-start.2
  217.8 1.0 copy-done.2
  218.7 0.0 copy-done.1
  218.7 1.8 fusion
  220.5 0.0 all-gather.6.cloned.1.call-update
  220.5 24.6 %all-gather.6.cloned.1.call-done = f32[1024,256]{1,0:T(8,128)} async-done(((f32[256,256]{1,0:T(8,128)}), f32[1024,256]{1,0:T(8,128)}) %all-gather.6.cloned.1.call-update) | async-done | bytes 1048592 | tf_op jit(solution)/shard_map/all_gather | solution.py:48
  245.2 1.3 reduce.1
  246.5 0.0 copy-done.3
  246.5 0.7 bitcast_subtract_fusion
  (1 shorter events, 0.0 us)
Async XLA Ops:
  7.2 88.3 %copy-start = (f32[1024,512]{1,0:T(8,128)S(1)}, f32[1024,512]{1,0:T(8,128)}, u32[]{:S(2)}) copy-start(f32[1024,512]{1,0:T(8,128)} %param.5) | copy-start | bytes 6291460
  7.2 88.3 %all-gather.4.cloned.1.call-start = ((), (), s32[]{:S(2)}) async-start(), calls=%async_computation.3 | async-start | bytes 9437184 | tf_op jit(solution)/shard_map/all_gather | solution.py:25
  10.6 153.1 %reduce-scatter.2.cloned.1.call-start = ((), (), s32[]{:S(2)}) async-start(), calls=%async_computation.4 | async-start | bytes 5242880 | tf_op jit(solution)/shard_map/reduce_scatter | solution.py:28
  112.4 132.8 %all-gather.6.cloned.1.call-start = ((), (), s32[]{:S(2)}) async-start(), calls=%async_computation.5 | async-start | bytes 1310720 | tf_op jit(solution)/shard_map/all_gather | solution.py:48
  196.4 22.3 %copy-start.1 = (f32[1,256,1024]{2,1,0:T(8,128)S(1)}, f32[1,256,1024]{2,1,0:T(8,128)}, u32[]{:S(2)}) copy-start(f32[1,256,1024]{2,1,0:T(8,128)} %param.4) | copy-start | bytes 3145732
  201.0 45.5 %copy-start.3 = (f32[1,256,256]{2,1,0:T(8,128)S(1)}, f32[1,256,256]{2,1,0:T(8,128)}, u32[]{:S(2)}) copy-start(f32[1,256,256]{2,1,0:T(8,128)} %param.7) | copy-start | bytes 786436
  217.8 1.0 copy-start.2
Sparse Core Ops, SparseCore 0:
  10.7 84.7 all-gather.3
  112.5 51.0 reduce-scatter.1
  220.6 24.4 all-gather.5
